TPU v7x, 512 devices: a whole 4x4x16 slice. The times are simulated.
512 devices in a mesh: tm: 32 (over z, y_hi), lat: 16 (over x, y_lo, core).
Axes of the slice: x: 4, y: 4 (y_hi: 2, y_lo: 2; y = y_hi * 2 + y_lo), z: 16, core: 2. Of those that a mesh axis runs over, the one named last changes fastest.
Arguments:
- controls: float32 [32, 3, 512, 1024], P('tm', None, 'lat'), may hold values from -3 to 3
- background: float32 [3, 512, 1024], P(None, 'lat'), may hold values from -3 to 3
- observations: float32 [32, 4, 512, 1024], P('tm', None, 'lat'), may hold values from -3 to 3
- obs_count: int32 [32, 4, 512, 1024], P('tm', None, 'lat'), may hold values from 0 to 3
Outputs:
- slid_controls: float32 [32, 3, 512, 1024], P('tm', None, 'lat')
- gradient: float32 [32, 3, 512, 1024], P('tm', None, 'lat')
- cost: float32 [], replicated
All inputs are finite; a program needn't handle non-finite values.
Results may differ from a plain program's by a relative error of at most 0.0001.
Values sent between devices are 32-bit elements; how exact they have to be, the bound alone decides.
A program may use at most 64 MiB of HBM per device.

v0:
```python
import jax
import jax.numpy as jnp
from jax import lax
from jax.sharding import Mesh
from jax.sharding import PartitionSpec as P

LAT = ("lat_0", "lat_1", "lat_2")
TM = ("tm_0", "tm_1")
TM_LAT = ("tm_0", "tm_1", "lat_0", "lat_1", "lat_2")


courant = 0.25
diffusion = 0.1
spin_scale = 0.3
obs_weight = 0.5
q_weight = 1.0
step_scale = 0.2
epsilon = 1e-06


def extended_2(cells, sides, width):
    for axis, dim in sides:
        count = lax.axis_size(axis)
        ends = count - 1
        head = lax.slice_in_dim(cells, 0, width, axis=dim)
        tail = lax.slice_in_dim(cells, cells.shape[dim] - width, cells.shape[dim], axis=dim)
        cells = jnp.concatenate(
            [
                lax.ppermute(tail, axis, [(i, (i + 1) % count) for i in range(ends)]),
                cells,
                lax.ppermute(head, axis, [((i + 1) % count, i) for i in range(ends)]),
            ],
            axis=dim,
        )
    return cells


def from_behind(block, axis, distance):
    devices = range(lax.axis_size(axis))
    route = [(i - distance, i) for i in devices if i - distance in devices]
    return lax.ppermute(block, axis, route)


def by_axis(x, axes):
    for axis in axes:
        x = lax.psum(x, axis)
    return x


def advance(extended, coriolis):
    center = extended[:, 1:-1]
    north = extended[:, 2:]
    south = extended[:, :-2]
    east = jnp.roll(center, -1, axis=2)
    west = jnp.roll(center, 1, axis=2)
    height, zonal, merid = (center[0], center[1], center[2])
    flux_east = east[1] * (1.0 + east[0])
    flux_west = west[1] * (1.0 + west[0])
    flux_north = north[2] * (1.0 + north[0])
    flux_south = south[2] * (1.0 + south[0])
    spread = north + south + east + west - 4.0 * center
    half = 0.5 * courant
    new_height = (
        height - half * (flux_east - flux_west + flux_north - flux_south) + diffusion * spread[0]
    )
    new_zonal = (
        zonal
        - half * (east[0] - west[0])
        + coriolis * merid
        - half * (zonal * (east[1] - west[1]) + merid * (north[1] - south[1]))
        + diffusion * spread[1]
    )
    new_merid = (
        merid
        - half * (north[0] - south[0])
        - coriolis * zonal
        - half * (zonal * (east[2] - west[2]) + merid * (north[2] - south[2]))
        + diffusion * spread[2]
    )
    return jnp.stack([new_height, new_zonal, new_merid])


def coriolis_rows(index, total):
    latitude = jnp.pi * ((index.astype(jnp.float32) + 0.5) / total - 0.5)
    return (spin_scale * jnp.sin(latitude))[:, None]


def section_rows(current, first, margin, total):
    count = current.shape[1] - 2
    index = first - margin + jnp.arange(count, dtype=jnp.int32)
    valid = ((index >= 0) & (index < total)).astype(jnp.float32)[:, None]
    return advance(current, coriolis_rows(index, total)) * valid


def add_rims(wide, got, width):
    inner = wide[:, width:-width]
    count = inner.shape[1]
    lower = jnp.pad(got[:, :width], ((0, 0), (0, count - width), (0, 0)))
    upper = jnp.pad(got[:, -width:], ((0, 0), (count - width, 0), (0, 0)))
    return inner + lower + upper


def with_height(grad, inject):
    return grad + jnp.concatenate([inject[None], jnp.zeros_like(grad[1:])], axis=0)


def forward_deep(state, weights, targets, first, total):
    rows = state.shape[1]
    steps = targets.shape[0]
    current = extended_2(state, ((LAT, 1),), steps)
    inputs = []
    resids = []
    cost = jnp.zeros((), jnp.float32)
    for section in range(steps):
        margin = steps - 1 - section
        inputs.append(current)
        current = section_rows(current, first, margin, total)
        resid = current[0, margin : margin + rows] - targets[section]
        resids.append(weights[section] * resid)
        cost = cost + 0.5 * jnp.sum(weights[section] * resid * resid)
    return (current, cost, inputs, resids)


def backward_deep(start_grad, inputs, resids, first, total):
    steps = len(inputs)
    grad = start_grad
    for section in reversed(range(steps)):
        margin = steps - 1 - section
        grad = with_height(grad, jnp.pad(resids[section], ((margin, margin), (0, 0))))
        outputs, pull = jax.vjp(
            lambda current: section_rows(current, first, margin, total), inputs[section]
        )
        grad = pull(grad)[0]
    rims = jnp.concatenate([grad[:, :steps], grad[:, -steps:]], axis=1)
    got = extended_2(rims, ((LAT, 1),), steps)
    return add_rims(grad, got, steps)


def per_device(controls, background, observations, obs_count):
    state = controls[0]
    rows = state.shape[1]
    total = rows * lax.axis_size(LAT)
    first = lax.axis_index(LAT) * rows
    position = lax.axis_index(TM)
    windows = lax.axis_size(TM)
    weights = obs_weight * obs_count[0].astype(jnp.float32)
    targets = observations[0]
    following = from_behind(state, TM, -1)
    final, obs_cost, inputs, resids = forward_deep(state, weights, targets, first, total)
    received = from_behind(final, TM, 1)
    previous = jnp.where(position == 0, background, received)
    misfit = state - previous
    weighted = q_weight * misfit
    local_cost = obs_cost + 0.5 * q_weight * jnp.sum(misfit * misfit)
    later = jnp.where(
        position == windows - 1, jnp.zeros_like(final), q_weight * (following - final)
    )
    cost_total = by_axis(local_cost, TM_LAT)
    adjoint = backward_deep(-later, inputs, resids, first, total)
    gradient = weighted + adjoint
    squares = jnp.sum(gradient * gradient)
    square_total = by_axis(squares, TM_LAT)
    entries = float(windows * lax.axis_size(LAT) * state.size)
    norm = jnp.sqrt(square_total / entries + epsilon)
    updated = state - step_scale * gradient / norm
    arriving = from_behind(updated, TM, -1)
    slid = jnp.where(position == windows - 1, final, arriving)
    return (slid[None], gradient[None], cost_total)


def solution(mesh):
    finer = Mesh(mesh.devices.reshape(16, 2, 4, 2, 2), ("tm_0", "tm_1", "lat_0", "lat_1", "lat_2"))
    return jax.shard_map(
        per_device,
        mesh=finer,
        in_specs=(
            P(TM, None, LAT, None),
            P(None, LAT, None),
            P(TM, None, LAT, None),
            P(TM, None, LAT, None),
        ),
        out_specs=(P(TM, None, LAT, None), P(TM, None, LAT, None), P()),
        check_vma=False,
    )
```

profile of v0, /device:TPU:1, one launch (start us, length us, event | category | flops | bytes accessed | tf_op | source)
XLA Modules:
  0.0 144.4 jit_solution(15232609845705432557)
XLA Ops:
  0.6 1.3 collective-permute-start.3
  1.9 1.0 fusion.121
  2.9 4.6 %collective-permute-start = (f32[3,4,1024]{2,1,0:T(4,128)S(1)}, f32[3,4,1024]{2,1,0:T(4,128)S(1)}, u32[]{:S(2)}, u32[]{:S(2)}) collective-permute-start(f32[3,4,1024]{2,1,0:T(4,128)S(1)} %get-tuple-element.254), channel_id=1, source_target_pairs={{0,1},{1,2},{2,3},{3,4},{4,5},{5,6},{6,7},{7,8},{8,9},{9,10},{10,1... | collective-permute-start | bytes 147464 | tf_op jit(solution)/shard_map/ppermute | solution.py:29
  7.5 5.5 %collective-permute-start.1 = (f32[3,4,1024]{2,1,0:T(4,128)S(1)}, f32[3,4,1024]{2,1,0:T(4,128)S(1)}, u32[]{:S(2)}, u32[]{:S(2)}) collective-permute-start(f32[3,4,1024]{2,1,0:T(4,128)S(1)} %get-tuple-element.255), channel_id=1, source_target_pairs={{1,0},{2,1},{3,2},{4,3},{5,4},{6,5},{7,6},{8,7},{9,8},{10,9},{11,1... | collective-permute-start | bytes 147464 | tf_op jit(solution)/shard_map/ppermute | solution.py:31
  13.8 1.9 %convert_multiply_fusion = f32[1,4,32,1024]{3,2,1,0:T(8,128)} fusion(s32[1,4,32,1024]{3,2,1,0:T(8,128)} %param.7), kind=kLoop, calls=%fused_computation.32 | loop fusion | flops 262144 | bytes 1048576 | tf_op jit(solution)/shard_map/mul | solution.py:146
  16.3 1.1 collective-permute-done
  17.4 0.7 collective-permute-done.1
  18.9 0.8 fusion.41
  20.9 0.8 fusion.38
  22.9 0.8 fusion.35
  25.3 0.8 fusion.63
  26.8 0.8 maximum_multiply_fusion.3
  27.6 4.7 %collective-permute-start.2 = (f32[3,32,1024]{2,1,0:T(8,128)}, f32[3,32,1024]{2,1,0:T(8,128)}, u32[]{:S(2)}, u32[]{:S(2)}) collective-permute-start(f32[3,32,1024]{2,1,0:T(8,128)} %maximum_multiply_fusion.3), channel_id=1, source_target_pairs={{0,16},{16,32},{32,48},{48,64},{64,80},{80,96},{96,112},{112,128},... | collective-permute-start | bytes 1179656 | tf_op jit(solution)/shard_map/ppermute | solution.py:41
  32.4 2.4 %fusion.50 = (f32[]{:T(128)}, f32[]{:T(128)}, f32[]{:T(128)}, f32[]{:T(128)}, f32[32,1024]{1,0:T(8,128)S(1)}, /*index=5*/f32[32,1024]{1,0:T(8,128)S(1)}, f32[32,1024]{1,0:T(8,128)}) fusion(f32[3,32,1024]{2,1,0:T(8,128)} %maximum_multiply_fusion.3, f32[1,4,32,1024]{3,2,1,0:T(8,128)S(1)} %copy-done.12, f32[1,4,32,1024]{3,2,1,0:T(8,128)S(1)} %copy-done.43, ...), kind=kLoop, calls=%fused_computation.234 | loop fusion | flops 524284 | bytes 1966096 | tf_op jit(solution)/shard_map/reduce_sum | solution.py:120
  38.6 0.9 pad_bitcast_fusion
  39.6 1.1 fusion.66
  40.8 1.2 add_multiply_fusion.3
  44.8 0.8 copy-done.48
  45.8 0.8 copy-done.5
  50.0 0.8 copy-done.1
  56.9 1.9 %collective-permute-start.4 = (f32[3,4,1024]{2,1,0:T(4,128)S(1)}, f32[3,4,1024]{2,1,0:T(4,128)S(1)}, u32[]{:S(2)}, u32[]{:S(2)}) collective-permute-start(f32[3,4,1024]{2,1,0:T(4,128)S(1)} %get-tuple-element.72), channel_id=1, source_target_pairs={{0,1},{1,2},{2,3},{3,4},{4,5},{5,6},{6,7},{7,8},{8,9},{9,10},{10,1... | collective-permute-start | bytes 147464 | tf_op jit(solution)/shard_map/ppermute | solution.py:29
  58.9 2.5 %collective-permute-start.5 = (f32[3,4,1024]{2,1,0:T(4,128)S(1)}, f32[3,4,1024]{2,1,0:T(4,128)S(1)}, u32[]{:S(2)}, u32[]{:S(2)}) collective-permute-start(f32[3,4,1024]{2,1,0:T(4,128)S(1)} %get-tuple-element.73), channel_id=1, source_target_pairs={{1,0},{2,1},{3,2},{4,3},{5,4},{6,5},{7,6},{8,7},{9,8},{10,9},{11,1... | collective-permute-start | bytes 147464 | tf_op jit(solution)/shard_map/ppermute | solution.py:31
  61.6 0.7 multiply_reduce_fusion
  63.0 1.4 collective-permute-done.5
  65.1 29.1 %all-reduce.137 = (f32[]{:T(128)}, f32[]{:T(128)}) all-reduce(f32[]{:T(128)} %get-tuple-element.22, f32[]{:T(128)S(6)} %add.788), channel_id=1, replica_groups=mesh['tm_0'=16,'tm_1'=2,'lat_0'=4,'lat_1'=2,'lat_2'=2] {'tm_0'}, use_global_device_ids=true, to_apply=%region_1.2 | all-reduce | flops 2 | bytes 16 | tf_op jit(solution)/shard_map/psum | solution.py:46
  94.2 6.1 %all-reduce.141 = (f32[]{:T(128)}, f32[]{:T(128)}) all-reduce(f32[]{:T(128)} %get-tuple-element.7, f32[]{:T(128)} %get-tuple-element.8), channel_id=1, replica_groups=mesh['tm_0'=16,'tm_1'=2,'lat_0'=4,'lat_1'=2,'lat_2'=2] {'tm_1'}, use_global_device_ids=true, to_apply=%region_2.3 | all-reduce | flops 2 | bytes 16 | tf_op jit(solution)/shard_map/psum | solution.py:46
  100.3 8.7 %all-reduce.138 = (f32[]{:T(128)}, f32[]{:T(128)}) all-reduce(f32[]{:T(128)} %get-tuple-element.15, f32[]{:T(128)} %get-tuple-element.16), channel_id=1, replica_groups=mesh['tm_0'=16,'tm_1'=2,'lat_0'=4,'lat_1'=2,'lat_2'=2] {'lat_0'}, use_global_device_ids=true, to_apply=%region_3.4 | all-reduce | flops 2 | bytes 16 | tf_op jit(solution)/shard_map/psum | solution.py:46
  109.0 4.5 %all-reduce.140 = (f32[]{:T(128)}, f32[]{:T(128)}) all-reduce(f32[]{:T(128)} %get-tuple-element.9, f32[]{:T(128)} %get-tuple-element.10), channel_id=1, replica_groups=mesh['tm_0'=16,'tm_1'=2,'lat_0'=4,'lat_1'=2,'lat_2'=2] {'lat_1'}, use_global_device_ids=true, to_apply=%region_4.5 | all-reduce | flops 2 | bytes 16 | tf_op jit(solution)/shard_map/psum | solution.py:46
  113.5 15.3 %all-reduce.139 = (f32[]{:T(128)}, f32[]{:T(128)}) all-reduce(f32[]{:T(128)} %get-tuple-element.13, f32[]{:T(128)} %get-tuple-element.14), channel_id=1, replica_groups=mesh['tm_0'=16,'tm_1'=2,'lat_0'=4,'lat_1'=2,'lat_2'=2] {'lat_2'}, use_global_device_ids=true, to_apply=%region_5.6 | all-reduce | flops 2 | bytes 16 | tf_op jit(solution)/shard_map/psum | solution.py:46
  129.5 1.4 collective-permute-start.6
  130.9 12.6 %collective-permute-done.6 = f32[3,32,1024]{2,1,0:T(8,128)S(1)} collective-permute-done((f32[3,32,1024]{2,1,0:T(8,128)S(1)}, f32[3,32,1024]{2,1,0:T(8,128)S(1)}, u32[]{:S(2)}, u32[]{:S(2)}) %collective-permute-start.6) | collective-permute-done | bytes 393248 | tf_op jit(solution)/shard_map/ppermute | solution.py:41
  143.6 0.9 select_bitcast_fusion
  (211 shorter events, 20.8 us)
Async XLA Ops:
  0.6 40.1 %collective-permute-start.3 = (f32[3,32,1024]{2,1,0:T(8,128)}, f32[3,32,1024]{2,1,0:T(8,128)}, u32[]{:S(2)}, u32[]{:S(2)}) collective-permute-start(f32[3,32,1024]{2,1,0:T(8,128)} %bitcast.92), channel_id=1, source_target_pairs={{16,0},{32,16},{48,32},{64,48},{80,64},{96,80},{112,96},{128,112},... | collective-permute-start | bytes 1179656 | tf_op jit(solution)/shard_map/ppermute | solution.py:41
  2.9 14.5 %collective-permute-start = (f32[3,4,1024]{2,1,0:T(4,128)S(1)}, f32[3,4,1024]{2,1,0:T(4,128)S(1)}, u32[]{:S(2)}, u32[]{:S(2)}) collective-permute-start(f32[3,4,1024]{2,1,0:T(4,128)S(1)} %get-tuple-element.254), channel_id=1, source_target_pairs={{0,1},{1,2},{2,3},{3,4},{4,5},{5,6},{6,7},{7,8},{8,9},{9,10},{10,1... | collective-permute-start | bytes 147464 | tf_op jit(solution)/shard_map/ppermute | solution.py:29
  7.5 10.6 %collective-permute-start.1 = (f32[3,4,1024]{2,1,0:T(4,128)S(1)}, f32[3,4,1024]{2,1,0:T(4,128)S(1)}, u32[]{:S(2)}, u32[]{:S(2)}) collective-permute-start(f32[3,4,1024]{2,1,0:T(4,128)S(1)} %get-tuple-element.255), channel_id=1, source_target_pairs={{1,0},{2,1},{3,2},{4,3},{5,4},{6,5},{7,6},{8,7},{9,8},{10,9},{11,1... | collective-permute-start | bytes 147464 | tf_op jit(solution)/shard_map/ppermute | solution.py:31
  13.0 6.9 %copy-start.61 = (f32[38]{0:T(128)}, f32[38]{0:T(128)S(1)}, u32[]{:S(2)}) copy-start(f32[38]{0:T(128)S(1)} %and_convert_fusion.3) | copy-start | bytes 460
  13.1 8.7 %copy-start.52 = (f32[36]{0:T(128)}, f32[36]{0:T(128)S(1)}, u32[]{:S(2)}) copy-start(f32[36]{0:T(128)S(1)} %sine_multiply_fusion.2) | copy-start | bytes 436
  13.1 8.9 %copy-start.63 = (f32[36]{0:T(128)}, f32[36]{0:T(128)S(1)}, u32[]{:S(2)}) copy-start(f32[36]{0:T(128)S(1)} %and_convert_fusion.2) | copy-start | bytes 436
  13.2 10.6 %copy-start.54 = (f32[34]{0:T(128)}, f32[34]{0:T(128)S(1)}, u32[]{:S(2)}) copy-start(f32[34]{0:T(128)S(1)} %sine_multiply_fusion.1) | copy-start | bytes 412
  13.2 10.8 %copy-start.65 = (f32[34]{0:T(128)}, f32[34]{0:T(128)S(1)}, u32[]{:S(2)}) copy-start(f32[34]{0:T(128)S(1)} %and_convert_fusion.1) | copy-start | bytes 412
  13.8 4.3 %copy-start.10 = (f32[1,3,32,1024]{3,2,1,0:T(8,128)S(1)}, f32[1,3,32,1024]{3,2,1,0:T(8,128)}, u32[]{:S(2)}) copy-start(f32[1,3,32,1024]{3,2,1,0:T(8,128)} %param.4) | copy-start | bytes 1179652
  18.2 1.5 %copy-start.13 = (f32[3,38,1]{2,1,0:T(8,128)}, f32[3,38,1]{2,1,0:T(8,128)S(1)}, u32[]{:S(2)}) copy-start(f32[3,38,1]{2,1,0:T(8,128)S(1)} %get-tuple-element.228) | copy-start | bytes 1372
  20.2 1.6 %copy-start.15 = (f32[3,36,1]{2,1,0:T(8,128)}, f32[3,36,1]{2,1,0:T(8,128)S(1)}, u32[]{:S(2)}) copy-start(f32[3,36,1]{2,1,0:T(8,128)S(1)} %get-tuple-element.223) | copy-start | bytes 1300
  20.2 1.6 %copy-start.17 = (f32[3,36,1]{2,1,0:T(8,128)}, f32[3,36,1]{2,1,0:T(8,128)S(1)}, u32[]{:S(2)}) copy-start(f32[3,36,1]{2,1,0:T(8,128)S(1)} %get-tuple-element.224) | copy-start | bytes 1300
  20.4 1.3 copy-start
  22.2 1.6 %copy-start.19 = (f32[3,34,1]{2,1,0:T(8,128)}, f32[3,34,1]{2,1,0:T(8,128)S(1)}, u32[]{:S(2)}) copy-start(f32[3,34,1]{2,1,0:T(8,128)S(1)} %get-tuple-element.219) | copy-start | bytes 1228
  22.2 1.5 %copy-start.21 = (f32[3,34,1]{2,1,0:T(8,128)}, f32[3,34,1]{2,1,0:T(8,128)S(1)}, u32[]{:S(2)}) copy-start(f32[3,34,1]{2,1,0:T(8,128)S(1)} %get-tuple-element.220) | copy-start | bytes 1228
  24.2 1.9 %copy-start.32 = (f32[3,32,1]{2,1,0:T(8,128)}, f32[3,32,1]{2,1,0:T(8,128)S(1)}, u32[]{:S(2)}) copy-start(f32[3,32,1]{2,1,0:T(8,128)S(1)} %get-tuple-element.216) | copy-start | bytes 1156
  24.4 1.7 %copy-start.6 = (f32[3,32,1023]{2,1,0:T(8,128)}, f32[3,32,1023]{2,1,0:T(8,128)S(1)}, u32[]{:S(2)}) copy-start(f32[3,32,1023]{2,1,0:T(8,128)S(1)} %get-tuple-element.213) | copy-start | bytes 1178500
  24.4 1.7 %copy-start.8 = (f32[3,32,1023]{2,1,0:T(8,128)}, f32[3,32,1023]{2,1,0:T(8,128)S(1)}, u32[]{:S(2)}) copy-start(f32[3,32,1023]{2,1,0:T(8,128)S(1)} %get-tuple-element.214) | copy-start | bytes 1178500
  26.2 6.2 %copy-start.43 = (f32[1,4,32,1024]{3,2,1,0:T(8,128)S(1)}, f32[1,4,32,1024]{3,2,1,0:T(8,128)}, u32[]{:S(2)}) copy-start(f32[1,4,32,1024]{3,2,1,0:T(8,128)} %param.6) | copy-start | bytes 1572868
  26.3 1.3 copy-start.26
  26.3 6.1 %copy-start.12 = (f32[1,4,32,1024]{3,2,1,0:T(8,128)S(1)}, f32[1,4,32,1024]{3,2,1,0:T(8,128)}, u32[]{:S(2)}) copy-start(f32[1,4,32,1024]{3,2,1,0:T(8,128)} %convert_multiply_fusion) | copy-start | bytes 1572868
  27.6 33.9 %collective-permute-start.2 = (f32[3,32,1024]{2,1,0:T(8,128)}, f32[3,32,1024]{2,1,0:T(8,128)}, u32[]{:S(2)}, u32[]{:S(2)}) collective-permute-start(f32[3,32,1024]{2,1,0:T(8,128)} %maximum_multiply_fusion.3), channel_id=1, source_target_pairs={{0,16},{16,32},{32,48},{48,64},{64,80},{80,96},{96,112},{112,128},... | collective-permute-start | bytes 1179656 | tf_op jit(solution)/shard_map/ppermute | solution.py:41
  56.9 6.1 %collective-permute-start.4 = (f32[3,4,1024]{2,1,0:T(4,128)S(1)}, f32[3,4,1024]{2,1,0:T(4,128)S(1)}, u32[]{:S(2)}, u32[]{:S(2)}) collective-permute-start(f32[3,4,1024]{2,1,0:T(4,128)S(1)} %get-tuple-element.72), channel_id=1, source_target_pairs={{0,1},{1,2},{2,3},{3,4},{4,5},{5,6},{6,7},{7,8},{8,9},{9,10},{10,1... | collective-permute-start | bytes 147464 | tf_op jit(solution)/shard_map/ppermute | solution.py:29
  58.8 2.7 %copy-start.11 = (f32[1,3,32,1024]{3,2,1,0:T(8,128)S(1)}, f32[1,3,32,1024]{3,2,1,0:T(8,128)}, u32[]{:S(2)}) copy-start(f32[1,3,32,1024]{3,2,1,0:T(8,128)} %param.4) | copy-start | bytes 1179652
  58.8 2.7 %copy-start.50 = (f32[3,32,1024]{2,1,0:T(8,128)S(1)}, f32[3,32,1024]{2,1,0:T(8,128)}, u32[]{:S(2)}) copy-start(f32[3,32,1024]{2,1,0:T(8,128)} %param.5) | copy-start | bytes 1179652
  58.9 5.5 %collective-permute-start.5 = (f32[3,4,1024]{2,1,0:T(4,128)S(1)}, f32[3,4,1024]{2,1,0:T(4,128)S(1)}, u32[]{:S(2)}, u32[]{:S(2)}) collective-permute-start(f32[3,4,1024]{2,1,0:T(4,128)S(1)} %get-tuple-element.73), channel_id=1, source_target_pairs={{1,0},{2,1},{3,2},{4,3},{5,4},{6,5},{7,6},{8,7},{9,8},{10,9},{11,1... | collective-permute-start | bytes 147464 | tf_op jit(solution)/shard_map/ppermute | solution.py:31
  65.1 64.4 %copy-start.34 = (f32[3,32,1024]{2,1,0:T(8,128)}, f32[3,32,1024]{2,1,0:T(8,128)S(1)}, u32[]{:S(2)}) copy-start(f32[3,32,1024]{2,1,0:T(8,128)S(1)} %get-tuple-element.23) | copy-start | bytes 1179652
  129.4 14.2 %copy-start.25 = (f32[1,32,1024]{2,1,0:T(8,128)S(1)}, f32[1,32,1024]{2,1,0:T(8,128)}, u32[]{:S(2)}) copy-start(f32[1,32,1024]{2,1,0:T(8,128)} %copy-done.23) | copy-start | bytes 393220
  129.4 14.1 %copy-start.28 = (f32[1,32,1024]{2,1,0:T(8,128)S(1)}, f32[1,32,1024]{2,1,0:T(8,128)}, u32[]{:S(2)}) copy-start(f32[1,32,1024]{2,1,0:T(8,128)} %copy-done.26) | copy-start | bytes 393220
  129.4 14.1 %copy-start.31 = (f32[1,32,1024]{2,1,0:T(8,128)S(1)}, f32[1,32,1024]{2,1,0:T(8,128)}, u32[]{:S(2)}) copy-start(f32[1,32,1024]{2,1,0:T(8,128)} %copy-done.29) | copy-start | bytes 393220
  129.4 14.1 %copy-start.60 = (f32[32]{0:T(128)S(1)}, f32[32]{0:T(128)}, u32[]{:S(2)}) copy-start(f32[32]{0:T(128)} %and_convert_fusion) | copy-start | bytes 388
  129.5 14.0 %collective-permute-start.6 = (f32[3,32,1024]{2,1,0:T(8,128)S(1)}, f32[3,32,1024]{2,1,0:T(8,128)S(1)}, u32[]{:S(2)}, u32[]{:S(2)}) collective-permute-start(f32[3,32,1024]{2,1,0:T(8,128)S(1)} %divide_subtract_fusion), channel_id=1, source_target_pairs={{16,0},{32,16},{48,32},{64,48},{80,64},{96,80},{112,96},{128,112},... | collective-permute-start | bytes 1179656 | tf_op jit(solution)/shard_map/ppermute | solution.py:41
  (42 other events, 41.4 us)
where the time goes:
time: 146 us; the launch traced here: 144 us
  blocking collectives  63.6 us (44%)
  other arithmetic  22.9 us (16%)
  starting transfers between devices  21.9 us (15%)
  waiting for transfers between devices  15.8 us (11%)
  local copies, waits for them, and re-layouts  14.5 us (10%)
  between operations  5.61 us (4%)
    psum x5, blocking collectives, by_axis(): x = lax.psum(x, axis)  63.6 us
    ppermute x3, waiting for transfers between devices, from_behind(): return lax.ppermute(block, axis, route)  12.6 us
    unnamed x134, local copies, waits for them, and re-layouts  9.05 us
    ppermute x2, starting transfers between devices, extended_2(): lax.ppermute(head, axis, [((i + 1) % count, i) for i in range(ends)])  7.99 us
    ppermute x3, starting transfers between devices, from_behind(): return lax.ppermute(block, axis, route)  7.44 us
    ppermute x2, starting transfers between devices, extended_2(): lax.ppermute(tail, axis, [(i, (i + 1) % count) for i in range(ends)])  6.5 us
    add x4, other arithmetic, advance(): merid - half * (north[0] - south[0]) - coriolis * zonal  3.31 us
    mul x8, other arithmetic, section_rows(): return advance(current, coriolis_rows(index, total)) * valid  2.94 us
  transfers between devices with their start and end apart: 7, of which 4 were waited for; matrix products, arithmetic and copies ran while one was open for 19% of the time, Pallas kernels for 0%

commit v1 on v0

v1 whole, which is shorter than its diff:
```python
import functools

import jax
import jax.numpy as jnp
from jax import lax
from jax.experimental import pallas as pl
from jax.experimental.pallas import tpu as pltpu
from jax.sharding import PartitionSpec as P

half = 0.125
diffusion = 0.1
spin_scale = 0.3
obs_weight = 0.5
step_scale = 0.2
epsilon = 1e-06

STEPS = 4
SUB, LANES = 8, 128
BLOCK = 8
MESH = pl.DeviceIdType.MESH


def east(x):
    near = pltpu.roll(x, LANES - 1, x.ndim - 1)
    far = pltpu.roll(near, SUB - 1, x.ndim - 2)
    lane = lax.broadcasted_iota(jnp.int32, x.shape, x.ndim - 1)
    return jnp.where(lane == LANES - 1, far, near)


def west(x):
    near = pltpu.roll(x, 1, x.ndim - 1)
    far = pltpu.roll(near, 1, x.ndim - 2)
    lane = lax.broadcasted_iota(jnp.int32, x.shape, x.ndim - 1)
    return jnp.where(lane == 0, far, near)


def kernel(
    windows,
    bands,
    rows,
    entries,
    x_hbm,
    bg_hbm,
    obs_hbm,
    cnt_hbm,
    slid_hbm,
    grad_hbm,
    cost_ref,
    xin,
    bg,
    obs,
    cnt,
    fol,
    S,
    L,
    WR,
    F,
    prev,
    adjn,
    edge,
    grad,
    slid,
    n1,
    n2,
    local,
    outs,
    send,
    recv,
    a_send,
    a_recv,
    n_sem,
    z_sem,
):
    tm, lat = lax.axis_index("tm"), lax.axis_index("lat")
    z, y_hi = tm // 2, tm % 2
    depth = windows // 2
    group = 2 * bands
    mine = y_hi * bands + lat
    total = rows * bands
    tiles = rows // SUB
    pad = STEPS + 1
    span = rows + 2 * STEPS
    plane = rows * SUB

    def at(t, l):
        return {"tm": t, "lat": l}

    def group_peer(d):
        g = lax.rem(mine + d, group)
        return at(2 * z + g // bands, g % bands)

    def z_peer(d):
        return at(2 * lax.rem(z + d + depth, depth) + y_hi, lat)

    has_prev, has_next = tm > 0, tm < windows - 1
    has_south, has_north = lat > 0, lat < bands - 1
    prev_dev, next_dev = at(tm - 1, lat), at(tm + 1, lat)
    south_dev, north_dev = at(tm, lat - 1), at(tm, lat + 1)

    loads = [
        pltpu.make_async_copy(x_hbm, xin, local.at[0]),
        pltpu.make_async_copy(obs_hbm, obs, local.at[1]),
        pltpu.make_async_copy(cnt_hbm, cnt, local.at[2]),
    ]
    load_bg = pltpu.make_async_copy(bg_hbm, bg, local.at[3])
    loads[0].start()
    barrier = pltpu.get_barrier_semaphore()

    def greet(d, carry):
        pl.semaphore_signal(barrier, inc=1, device_id=group_peer(d), device_id_type=MESH)
        return carry

    def greet_dev(dev):
        pl.semaphore_signal(barrier, inc=1, device_id=dev, device_id_type=MESH)

    greet_dev(at(2 * lax.rem(z + 2 * y_hi - 1 + depth, depth) + 1 - y_hi, lat))
    greet_dev(z_peer(1))
    greet_dev(z_peer(-1))
    lax.fori_loop(1, group, greet, 0)
    loads[1].start()
    loads[2].start()
    pl.when(tm == 0)(lambda: load_bg.start())

    row_tile = jnp.zeros((SUB, LANES), jnp.float32)

    def table(t, carry):
        index = lax.broadcasted_iota(jnp.int32, (SUB, LANES), 0) + (t * SUB + lat * rows - pad)
        f = spin_scale * jnp.sin(jnp.pi * ((index.astype(jnp.float32) + 0.5) / total - 0.5))
        for r in range(SUB):
            F[t * SUB + r] = jnp.broadcast_to(f[r : r + 1], (SUB, LANES))
        return carry

    lax.fori_loop(0, (span + 2 + SUB - 1) // SUB, table, 0)
    for c in range(3):
        for j in range(STEPS):
            S[j, c, 0] = row_tile
            S[j, c, span + 1] = row_tile
        for p in range(2):
            L[p, c, 0] = row_tile
            L[p, c, span + 1] = row_tile
        for b in range(1, pad):
            L[0, c, b] = row_tile
            L[0, c, b + rows + STEPS] = row_tile

    def zero_rows(ref, first):
        for c in range(3):
            for b in range(STEPS):
                ref[c, first + b] = row_tile

    def poles(ref):
        pl.when(lat == 0)(lambda: zero_rows(ref, 1))
        pl.when(lat == bands - 1)(lambda: zero_rows(ref, pad + rows))

    def tile_row(c, t, r):
        return pl.ds(c * plane + t * SUB * SUB + r, SUB, stride=SUB)

    def per_row(fn, carry=0):
        def body(t, carry):
            for r in range(SUB):
                carry = fn(t, r, carry)
            return carry

        return lax.fori_loop(0, tiles, body, carry)

    poles(S.at[0])
    loads[0].wait()

    def unpack(t, r, carry):
        for c in range(3):
            S[0, c, pad + t * SUB + r] = xin[tile_row(c, t, r), :]
        return carry

    per_row(unpack)
    pl.semaphore_wait(barrier, group - 1 + 3)

    def remote(src, dst, k, dev):
        return pltpu.make_async_remote_copy(
            src_ref=src,
            dst_ref=dst,
            send_sem=send.at[k],
            recv_sem=recv.at[k],
            device_id=dev,
            device_id_type=MESH,
        )

    top = pl.ds(pad + rows - STEPS, STEPS)
    low = pl.ds(pad, STEPS)
    above = pl.ds(pad + rows, STEPS)
    below = pl.ds(1, STEPS)
    halo_up = remote(S.at[0, :, top], S.at[0, :, below], 0, north_dev)
    halo_down = remote(S.at[0, :, low], S.at[0, :, above], 1, south_dev)
    control = remote(xin, fol, 2, prev_dev)
    center = pl.ds(pad, rows)
    final = [remote(S.at[STEPS, c, center], prev.at[c], 3 + c, next_dev) for c in range(3)]
    out = 0
    edge_up = remote(L.at[out, :, above], edge.at[0], 6, north_dev)
    edge_down = remote(L.at[out, :, below], edge.at[1], 7, south_dev)

    pl.when(has_north)(lambda: halo_up.start())
    pl.when(has_south)(lambda: halo_down.start())
    pl.when(has_prev)(lambda: control.start())

    def z_signal(k):
        for d in (2**k, -(2**k)):
            pl.semaphore_signal(
                z_sem.at[k], inc=1, device_id=z_peer(d), device_id_type=MESH
            )

    z_signal(0)
    pl.when(has_south)(lambda: halo_up.wait_recv())
    pl.when(has_north)(lambda: halo_down.wait_recv())

    def forward(j):
        def block(t, carry):
            b = 1 + t * BLOCK

            def rows_at(c, shift):
                return S[j, c, pl.ds(b + shift, BLOCK)]

            h, u, v = (rows_at(c, 0) for c in range(3))
            hn, un, vn = (rows_at(c, 1) for c in range(3))
            hs, us, vs = (rows_at(c, -1) for c in range(3))
            he, ue, ve = east(h), east(u), east(v)
            hw, uw, vw = west(h), west(u), west(v)
            f = F[pl.ds(b, BLOCK)]
            flux = ue * (1.0 + he) - uw * (1.0 + hw) + vn * (1.0 + hn) - vs * (1.0 + hs)
            S[j + 1, 0, pl.ds(b, BLOCK)] = (
                h - half * flux + diffusion * (hn + hs + he + hw - 4.0 * h)
            )
            S[j + 1, 1, pl.ds(b, BLOCK)] = (
                u
                - half * (he - hw + u * (ue - uw) + v * (un - us))
                + f * v
                + diffusion * (un + us + ue + uw - 4.0 * u)
            )
            S[j + 1, 2, pl.ds(b, BLOCK)] = (
                v
                - half * (hn - hs + u * (ve - vw) + v * (vn - vs))
                - f * u
                + diffusion * (vn + vs + ve + vw - 4.0 * v)
            )
            return carry

        lax.fori_loop(0, span // BLOCK, block, 0)
        poles(S.at[j + 1])

    for j in range(STEPS):
        forward(j)

    @pl.when(has_next)
    def _():
        for c in range(3):
            final[c].start()

    pl.semaphore_wait(z_sem.at[0], 2)
    z_signal(1)

    loads[1].wait()
    loads[2].wait()
    zero = jnp.zeros((SUB, LANES), jnp.float32)

    def observe(j):
        def fn(t, r, cost):
            resid = S[j + 1, 0, pad + t * SUB + r] - obs[tile_row(j, t, r), :]
            weighted = obs_weight * cnt[tile_row(j, t, r), :].astype(jnp.float32) * resid
            WR[j, t * SUB + r] = weighted
            return cost + weighted * resid

        return fn

    cost = zero
    for j in range(STEPS):
        cost = per_row(observe(j), cost)

    pl.semaphore_wait(z_sem.at[1], 2)
    z_signal(2)

    @pl.when(has_next)
    def _():
        control.wait_recv()

        def start(t, r, carry):
            i = t * SUB + r
            for c in range(3):
                back = S[STEPS, c, pad + i] - fol[tile_row(c, t, r), :]
                if c == 0:
                    back = back + WR[STEPS - 1, i]
                L[0, c, pad + i] = back
            return carry

        per_row(start)

    @pl.when(jnp.logical_not(has_next))
    def _():
        def start(t, r, carry):
            i = t * SUB + r
            L[0, 0, pad + i] = WR[STEPS - 1, i]
            L[0, 1, pad + i] = row_tile
            L[0, 2, pad + i] = row_tile
            return carry

        per_row(start)

    def backward(j, p):
        def block(t, carry):
            b = 1 + t * BLOCK

            def grads(c, shift):
                return L[p, c, pl.ds(b + shift, BLOCK)]

            def state(c, shift):
                return S[j, c, pl.ds(b + shift, BLOCK)]

            H, U, V = (grads(c, 0) for c in range(3))
            HN, UN, VN = (grads(c, 1) for c in range(3))
            HS, US, VS = (grads(c, -1) for c in range(3))
            HE, UE, VE = east(H), east(U), east(V)
            HW, UW, VW = west(H), west(U), west(V)
            h, u, v = (state(c, 0) for c in range(3))
            un, vn = state(1, 1), state(2, 1)
            us, vs = state(1, -1), state(2, -1)
            ue, ve = east(u), east(v)
            uw, vw = west(u), west(v)
            f = F[pl.ds(b, BLOCK)]
            along, across = HE - HW, HN - HS
            thick = 1.0 + h
            L[1 - p, 0, pl.ds(b, BLOCK)] = (
                H
                + half * (along * u + across * v + (UE - UW) + (VN - VS))
                + diffusion * (HN + HS + HE + HW - 4.0 * H)
            )
            L[1 - p, 1, pl.ds(b, BLOCK)] = (
                U
                - f * V
                + half
                * (
                    along * thick
                    - U * (ue - uw)
                    - V * (ve - vw)
                    + (UE * ue - UW * uw)
                    + (UN * vn - US * vs)
                )
                + diffusion * (UN + US + UE + UW - 4.0 * U)
            )
            L[1 - p, 2, pl.ds(b, BLOCK)] = (
                V
                + f * U
                + half
                * (
                    across * thick
                    - U * (un - us)
                    - V * (vn - vs)
                    + (VE * ue - VW * uw)
                    + (VN * vn - VS * vs)
                )
                + diffusion * (VN + VS + VE + VW - 4.0 * V)
            )
            return carry

        lax.fori_loop(0, span // BLOCK, block, 0)
        if j > 0:

            def inject(t, r, carry):
                i = t * SUB + r
                L[1 - p, 0, pad + i] = L[1 - p, 0, pad + i] + WR[j - 1, i]
                return carry

            per_row(inject)
            poles(L.at[1 - p])

    p = 0
    for j in reversed(range(STEPS)):
        backward(j, p)
        p = 1 - p

    pl.when(has_north)(lambda: edge_up.start())
    pl.when(has_south)(lambda: edge_down.start())

    @pl.when(tm == 0)
    def _():
        load_bg.wait()

        def fn(t, r, carry):
            for c in range(3):
                prev[c, t * SUB + r] = bg[tile_row(c, t, r), :]
            return carry

        per_row(fn)

    @pl.when(has_south)
    def _():
        edge_up.wait_recv()
        for c in range(3):
            L[p, c, low] = L[p, c, low] + edge[0, c]

    @pl.when(has_north)
    def _():
        edge_down.wait_recv()
        for c in range(3):
            L[p, c, top] = L[p, c, top] + edge[1, c]

    @pl.when(has_prev)
    def _():
        for c in range(3):
            final[c].wait_recv()

    def gradient(t, r, carry):
        squares, cost = carry
        i = t * SUB + r
        for c in range(3):
            misfit = S[0, c, pad + i] - prev[c, i]
            g = misfit + L[p, c, pad + i]
            grad[tile_row(c, t, r), :] = g
            squares = squares + g * g
            cost = cost + misfit * misfit
        return squares, cost

    squares, cost = per_row(gradient, (zero, cost))

    def fold(x):
        x = jnp.sum(x, axis=0, keepdims=True)
        return x + pltpu.roll(x, LANES // 2, 1)

    lane = lax.broadcasted_iota(jnp.int32, (1, LANES), 1)
    n1[mine] = jnp.where(lane < LANES // 2, fold(squares), fold(cost))
    pl.semaphore_wait(z_sem.at[2], 2)

    def share(ref, slot, k, dev):
        return pltpu.make_async_remote_copy(
            src_ref=ref.at[slot],
            dst_ref=ref.at[slot],
            send_sem=n_sem.at[k, 0],
            recv_sem=n_sem.at[k, 1],
            device_id=dev,
            device_id_type=MESH,
        )

    def share1(d, carry):
        share(n1, mine, 0, group_peer(d)).start()
        return carry

    lax.fori_loop(1, group, share1, 0)

    pieces = []
    for q in range(2):
        for c in range(3):
            k = len(pieces)
            part = pl.ds(q * rows // 2, rows // 2)
            pieces.append(
                pltpu.make_async_remote_copy(
                    src_ref=L.at[p, c, pl.ds(pad + q * rows // 2, rows // 2)],
                    dst_ref=adjn.at[c, part],
                    send_sem=a_send.at[k],
                    recv_sem=a_recv.at[k],
                    device_id=prev_dev,
                    device_id_type=MESH,
                )
            )

    @pl.when(has_prev)
    def _():
        for piece in pieces[:3]:
            piece.start()

    store_grad = pltpu.make_async_copy(grad, grad_hbm, outs.at[0])
    store_grad.start()

    def settle(ref, count, k):
        many = pltpu.make_async_remote_copy(
            src_ref=ref.at[pl.ds(0, count)],
            dst_ref=ref.at[pl.ds(0, count)],
            send_sem=n_sem.at[k, 0],
            recv_sem=n_sem.at[k, 1],
            device_id=group_peer(1),
            device_id_type=MESH,
        )
        return many

    settle(n1, group - 1, 0).wait_recv()
    n2[z] = jnp.sum(n1[...], axis=0)

    def share2(d, carry):
        share(n2, z, 1, z_peer(d)).start()
        return carry

    lax.fori_loop(1, depth, share2, 0)

    @pl.when(has_prev)
    def _():
        for piece in pieces[3:]:
            piece.start()

    settle(n2, depth - 1, 1).wait_recv()
    sums = jnp.sum(n2[...], axis=0)
    square_total = jnp.sum(jnp.where(lane < LANES // 2, sums, 0.0), axis=1, keepdims=True)
    cost_total = jnp.sum(jnp.where(lane < LANES // 2, 0.0, sums), axis=1, keepdims=True)
    cost_ref[...] = jnp.broadcast_to(0.5 * cost_total, (SUB, LANES))
    scale = step_scale / jnp.sqrt(square_total / entries + epsilon)
    scale = jnp.broadcast_to(scale, (SUB, LANES))

    @pl.when(has_next)
    def _():
        for piece in pieces:
            piece.wait_recv()

        def fn(t, r, carry):
            i = t * SUB + r
            for c in range(3):
                control = fol[tile_row(c, t, r), :]
                g = (control - S[STEPS, c, pad + i]) + adjn[c, i]
                slid[tile_row(c, t, r), :] = control - scale * g
            return carry

        per_row(fn)

    @pl.when(jnp.logical_not(has_next))
    def _():
        def fn(t, r, carry):
            for c in range(3):
                slid[tile_row(c, t, r), :] = S[STEPS, c, pad + t * SUB + r]
            return carry

        per_row(fn)

    store_slid = pltpu.make_async_copy(slid, slid_hbm, outs.at[1])
    store_slid.start()
    pl.when(has_north)(lambda: halo_up.wait_send())
    pl.when(has_south)(lambda: halo_down.wait_send())
    pl.when(has_north)(lambda: edge_up.wait_send())
    pl.when(has_south)(lambda: edge_down.wait_send())

    @pl.when(has_next)
    def _():
        for c in range(3):
            final[c].wait_send()

    @pl.when(has_prev)
    def _():
        control.wait_send()
        for piece in pieces:
            piece.wait_send()

    settle(n1, group - 1, 0).wait_send()
    settle(n2, depth - 1, 1).wait_send()
    store_grad.wait()
    store_slid.wait()


def to_tiles(x):
    c, rows, lon = x.shape
    x = x.reshape(c, rows // SUB, SUB, lon // LANES, LANES)
    return x.transpose(0, 1, 3, 2, 4).reshape(c * rows * lon // LANES, LANES)


def from_tiles(x, rows, lon):
    x = x.reshape(-1, rows // SUB, lon // LANES, SUB, LANES)
    return x.transpose(0, 1, 3, 2, 4).reshape(-1, rows, lon)


def per_device(controls, background, observations, obs_count):
    rows, lon = controls.shape[2:]
    windows, bands = lax.axis_size("tm"), lax.axis_size("lat")
    entries = float(windows * bands * controls[0].size)
    n = 3 * rows * lon // LANES
    m = STEPS * rows * lon // LANES
    high = rows + 2 * STEPS + 2
    vmem = lambda *shape: pltpu.VMEM(shape, jnp.float32)
    dma = pltpu.SemaphoreType.DMA
    shape = jax.ShapeDtypeStruct((n, LANES), jnp.float32)
    slid, grad, cost = pl.pallas_call(
        functools.partial(kernel, windows, bands, rows, entries),
        out_shape=(shape, shape, jax.ShapeDtypeStruct((SUB, LANES), jnp.float32)),
        in_specs=[pl.BlockSpec(memory_space=pl.ANY)] * 4,
        out_specs=(
            pl.BlockSpec(memory_space=pl.ANY),
            pl.BlockSpec(memory_space=pl.ANY),
            pl.BlockSpec(memory_space=pltpu.VMEM),
        ),
        scratch_shapes=[
            vmem(n, LANES),
            vmem(n, LANES),
            vmem(m, LANES),
            pltpu.VMEM((m, LANES), jnp.int32),
            vmem(n, LANES),
            vmem(STEPS + 1, 3, high, SUB, LANES),
            vmem(2, 3, high, SUB, LANES),
            vmem(STEPS, rows, SUB, LANES),
            vmem((high + SUB - 1) // SUB * SUB, SUB, LANES),
            vmem(3, rows, SUB, LANES),
            vmem(3, rows, SUB, LANES),
            vmem(2, 3, STEPS, SUB, LANES),
            vmem(n, LANES),
            vmem(n, LANES),
            vmem(2 * bands, 1, LANES),
            vmem(windows // 2, 1, LANES),
            dma((4,)),
            dma((2,)),
            dma((8,)),
            dma((8,)),
            dma((6,)),
            dma((6,)),
            dma((2, 2)),
            pltpu.SemaphoreType.REGULAR((3,)),
        ],
        compiler_params=pltpu.CompilerParams(collective_id=0, has_side_effects=True),
    )(
        to_tiles(controls[0]),
        to_tiles(background),
        to_tiles(observations[0]),
        to_tiles(obs_count[0]),
    )
    return (
        from_tiles(slid, rows, lon)[None],
        from_tiles(grad, rows, lon)[None],
        cost[0, 0],
    )


def solution(mesh):
    spec = P("tm", None, "lat", None)
    return jax.shard_map(
        per_device,
        mesh=mesh,
        in_specs=(spec, P(None, "lat", None), spec, spec),
        out_specs=(spec, spec, P()),
        check_vma=False,
    )
```

time: 146 us -> 62.6 us (0.43)
  blocking collectives: 63.6 us -> 0 us
  Pallas kernels: 0 us -> 58 us
  other arithmetic: 22.9 us -> 0 us
  starting transfers between devices: 21.9 us -> 0 us
  waiting for transfers between devices: 15.8 us -> 0 us
  local copies, waits for them, and re-layouts: 14.5 us -> 3.75 us
  between operations: 5.61 us -> 0.64 us
    psum x5 -> x0, blocking collectives: 63.6 us -> none  [by_axis(): x = lax.psum(x, axis)]
    pallas_call x0 -> x1, Pallas kernels: none -> 58 us  [per_device(): pl.pallas_call(functools.partial(kernel, windows, bands, rows, entries),...]
    ppermute x7 -> x0, starting transfers between devices: 21.9 us -> none  [the longest x2 7.99 us: extended_2(): lax.ppermute(head, axis, [((i + 1) % count, i) for i in range(ends)])]
    ppermute x7 -> x0, waiting for transfers between devices: 15.8 us -> none  [the longest x3 12.6 us: from_behind(): return lax.ppermute(block, axis, route)]
    mul x18 -> x0, other arithmetic: 7.2 us -> none  [the longest x8 2.94 us: section_rows(): return advance(current, coriolis_rows(index, total)) * valid]
    unnamed x134 -> x4, local copies, waits for them, and re-layouts: 9.05 us -> 2.57 us
    add x12 -> x0, other arithmetic: 4.75 us -> none  [the longest x4 3.31 us: advance(): merid - half * (north[0] - south[0]) - coriolis * zonal]
    reduce_sum x3 -> x0, other arithmetic: 3.82 us -> none  [the longest x1 2.38 us: forward_deep(): cost = cost + 0.5 * jnp.sum(weights[section] * resid * resid)]
  transfers between devices with their start and end apart: 7 -> 0, of which waited for: 4 -> 0; matrix products, arithmetic and copies ran while one was open for 19% -> 0% of each run, Pallas kernels for 0% -> 0%
where the time goes in v1:
time: 62.6 us; the launch traced here: 62.4 us
  Pallas kernels  58 us (93%)
  local copies, waits for them, and re-layouts  3.75 us (6%)
  between operations  0.64 us (1%)
    pallas_call x1, Pallas kernels, per_device(): pl.pallas_call(functools.partial(kernel, windows, bands, rows, entries),...  58 us
    unnamed x4, local copies, waits for them, and re-layouts  2.57 us

profile of v1, /device:TPU:1, one launch (start us, length us, event | category | flops | bytes accessed | tf_op | source)
XLA Modules:
  0.0 62.4 jit_solution(16641187747977666080)
XLA Ops:
  0.6 58.0 %shard_map.67 = (f32[768,128]{1,0:T(8,128)}, f32[768,128]{1,0:T(8,128)}, f32[8,128]{1,0:T(8,128)}) custom-call(f32[768,128]{1,0:T(8,128)} %bitcast.33, f32[768,128]{1,0:T(8,128)} %bitcast.34, f32[1024,128]{1,0:T(8,128)} %bitcast.31, s32[1024,128]{1,0:T(8,128)} %bitcast.32), custom_call_target="tpu_custom_call" | custom-call | tf_op jit(solution)/shard_map/pallas_call | solution.py:570
  58.7 1.2 %slice.3 = f32[1,1]{1,0:T(1,128)} slice(f32[8,128]{1,0:T(8,128)} %get-tuple-element.8), slice={[0:1], [0:1]} | slice | bytes 8 | tf_op jit(solution)/shard_map/slice | solution.py:615
  59.9 0.0 copy-start
  59.9 1.8 %copy.9 = f32[1,3,32,1024]{3,2,1,0:T(8,128)} copy(f32[1,3,32,1024]{3,2,1,0:T(8,128)} %bitcast.36) | data formatting | bytes 786432
  61.7 0.0 copy-done
  61.7 0.7 %copy.10 = f32[1,3,32,1024]{3,2,1,0:T(8,128)} copy(f32[1,3,32,1024]{3,2,1,0:T(8,128)S(1)} %bitcast.35) | data formatting | bytes 786432
Async XLA Ops:
  59.9 1.8 %copy-start = (f32[768,128]{1,0:T(8,128)S(1)}, f32[768,128]{1,0:T(8,128)}, u32[]{:S(2)}) copy-start(f32[768,128]{1,0:T(8,128)} %get-tuple-element.7) | copy-start | bytes 1179652

commit v2 on v1

--- a/solution.py
+++ b/solution.py
@@ -16,7 +16,8 @@
 
 STEPS = 4
 SUB, LANES = 8, 128
-BLOCK = 8
+BLOCK = 20
+EARLY, MIDDLE = 0, 3
 MESH = pl.DeviceIdType.MESH
 
 
@@ -43,8 +44,8 @@
     bg_hbm,
     obs_hbm,
     cnt_hbm,
-    slid_hbm,
-    grad_hbm,
+    slid,
+    grad,
     cost_ref,
     xin,
     bg,
@@ -58,14 +59,14 @@
     prev,
     adjn,
     edge,
-    grad,
-    slid,
     n1,
     n2,
+    n3,
     local,
-    outs,
     send,
     recv,
+    f_send,
+    f_recv,
     a_send,
     a_recv,
     n_sem,
@@ -74,8 +75,8 @@
     tm, lat = lax.axis_index("tm"), lax.axis_index("lat")
     z, y_hi = tm // 2, tm % 2
     depth = windows // 2
-    group = 2 * bands
-    mine = y_hi * bands + lat
+    x, y_lo, core = lat // 4, lat // 2 % 2, lat % 2
+    y = 2 * y_hi + y_lo
     total = rows * bands
     tiles = rows // SUB
     pad = STEPS + 1
@@ -85,9 +86,16 @@
     def at(t, l):
         return {"tm": t, "lat": l}
 
-    def group_peer(d):
-        g = lax.rem(mine + d, group)
-        return at(2 * z + g // bands, g % bands)
+    across = bands // 2
+    slot = 2 * x + core
+
+    def x_peer(d):
+        i = lax.rem(slot + d, across)
+        return at(tm, 4 * (i // 2) + 2 * y_lo + i % 2)
+
+    def y_peer(d):
+        i = lax.rem(y + d, 4)
+        return at(2 * z + i // 2, 4 * x + 2 * (i % 2) + core)
 
     def z_peer(d):
         return at(2 * lax.rem(z + d + depth, depth) + y_hi, lat)
@@ -106,17 +114,20 @@
     loads[0].start()
     barrier = pltpu.get_barrier_semaphore()
 
-    def greet(d, carry):
-        pl.semaphore_signal(barrier, inc=1, device_id=group_peer(d), device_id_type=MESH)
-        return carry
-
-    def greet_dev(dev):
+    def greet(dev):
         pl.semaphore_signal(barrier, inc=1, device_id=dev, device_id_type=MESH)
 
-    greet_dev(at(2 * lax.rem(z + 2 * y_hi - 1 + depth, depth) + 1 - y_hi, lat))
-    greet_dev(z_peer(1))
-    greet_dev(z_peer(-1))
-    lax.fori_loop(1, group, greet, 0)
+    z_below, z_above = z > 0, z < depth - 1
+    pl.when(z_below & (y_hi == 0))(lambda: greet(prev_dev))
+    pl.when(z_above & (y_hi == 1))(lambda: greet(next_dev))
+    pl.when(z_below)(lambda: greet(z_peer(-1)))
+    pl.when(z_above)(lambda: greet(z_peer(1)))
+    greet(at(tm, lax.rem(lat + 1, bands)))
+    greet(at(tm, lax.rem(lat + bands - 1, bands)))
+    for d in range(1, 4):
+        greet(y_peer(d))
+    for d in range(1, across):
+        greet(x_peer(d))
     loads[1].start()
     loads[2].start()
     pl.when(tm == 0)(lambda: load_bg.start())
@@ -171,7 +182,10 @@
         return carry
 
     per_row(unpack)
-    pl.semaphore_wait(barrier, group - 1 + 3)
+    before = (z + depth - 1) // depth
+    after = (2 * depth - 2 - z) // depth
+    facing = (1 - y_hi) * before + y_hi * after
+    pl.semaphore_wait(barrier, 2 + 3 + across - 1 + before + after + facing)
 
     def remote(src, dst, k, dev):
         return pltpu.make_async_remote_copy(
@@ -190,21 +204,41 @@
     halo_up = remote(S.at[0, :, top], S.at[0, :, below], 0, north_dev)
     halo_down = remote(S.at[0, :, low], S.at[0, :, above], 1, south_dev)
     control = remote(xin, fol, 2, prev_dev)
-    center = pl.ds(pad, rows)
-    final = [remote(S.at[STEPS, c, center], prev.at[c], 3 + c, next_dev) for c in range(3)]
+    final = []
+    for q in range(2):
+        for c in range(3):
+            k = len(final)
+            final.append(
+                pltpu.make_async_remote_copy(
+                    src_ref=S.at[STEPS, c, pl.ds(pad + q * rows // 2, rows // 2)],
+                    dst_ref=prev.at[c, pl.ds(q * rows // 2, rows // 2)],
+                    send_sem=f_send.at[k],
+                    recv_sem=f_recv.at[k],
+                    device_id=next_dev,
+                    device_id_type=MESH,
+                )
+            )
     out = 0
-    edge_up = remote(L.at[out, :, above], edge.at[0], 6, north_dev)
-    edge_down = remote(L.at[out, :, below], edge.at[1], 7, south_dev)
+    edge_up = remote(L.at[out, :, above], edge.at[0], 3, north_dev)
+    edge_down = remote(L.at[out, :, below], edge.at[1], 4, south_dev)
 
     pl.when(has_north)(lambda: halo_up.start())
     pl.when(has_south)(lambda: halo_down.start())
     pl.when(has_prev)(lambda: control.start())
 
     def z_signal(k):
-        for d in (2**k, -(2**k)):
-            pl.semaphore_signal(
-                z_sem.at[k], inc=1, device_id=z_peer(d), device_id_type=MESH
-            )
+        d = 2**k
+        for exists, e in ((z >= d, -d), (z < depth - d, d)):
+
+            @pl.when(exists)
+            def _():
+                pl.semaphore_signal(
+                    z_sem.at[k], inc=1, device_id=z_peer(e), device_id_type=MESH
+                )
+
+    def z_wait(k):
+        d = 2**k
+        pl.semaphore_wait(z_sem.at[k], (z + depth - d) // depth + (2 * depth - 1 - d - z) // depth)
 
     z_signal(0)
     pl.when(has_south)(lambda: halo_up.wait_recv())
@@ -249,10 +283,10 @@
 
     @pl.when(has_next)
     def _():
-        for c in range(3):
-            final[c].start()
-
-    pl.semaphore_wait(z_sem.at[0], 2)
+        for piece in final[:EARLY]:
+            piece.start()
+
+    z_wait(0)
     z_signal(1)
 
     loads[1].wait()
@@ -272,12 +306,11 @@
     for j in range(STEPS):
         cost = per_row(observe(j), cost)
 
-    pl.semaphore_wait(z_sem.at[1], 2)
-    z_signal(2)
-
     @pl.when(has_next)
     def _():
         control.wait_recv()
+        for piece in final[EARLY:MIDDLE]:
+            piece.start()
 
         def start(t, r, carry):
             i = t * SUB + r
@@ -376,6 +409,14 @@
     pl.when(has_north)(lambda: edge_up.start())
     pl.when(has_south)(lambda: edge_down.start())
 
+    @pl.when(has_next)
+    def _():
+        for piece in final[MIDDLE:]:
+            piece.start()
+
+    z_wait(1)
+    z_signal(2)
+
     @pl.when(tm == 0)
     def _():
         load_bg.wait()
@@ -401,8 +442,8 @@
 
     @pl.when(has_prev)
     def _():
-        for c in range(3):
-            final[c].wait_recv()
+        for piece in final:
+            piece.wait_recv()
 
     def gradient(t, r, carry):
         squares, cost = carry
@@ -422,24 +463,22 @@
         return x + pltpu.roll(x, LANES // 2, 1)
 
     lane = lax.broadcasted_iota(jnp.int32, (1, LANES), 1)
-    n1[mine] = jnp.where(lane < LANES // 2, fold(squares), fold(cost))
-    pl.semaphore_wait(z_sem.at[2], 2)
-
-    def share(ref, slot, k, dev):
+    z_wait(2)
+    z_signal(3)
+    n1[slot] = jnp.where(lane < LANES // 2, fold(squares), fold(cost))
+
+    def share(ref, i, k, dev):
         return pltpu.make_async_remote_copy(
-            src_ref=ref.at[slot],
-            dst_ref=ref.at[slot],
+            src_ref=ref.at[i],
+            dst_ref=ref.at[i],
             send_sem=n_sem.at[k, 0],
             recv_sem=n_sem.at[k, 1],
             device_id=dev,
             device_id_type=MESH,
         )
 
-    def share1(d, carry):
-        share(n1, mine, 0, group_peer(d)).start()
-        return carry
-
-    lax.fori_loop(1, group, share1, 0)
+    for d in range(1, across):
+        share(n1, slot, 0, x_peer(d)).start()
 
     pieces = []
     for q in range(2):
@@ -459,11 +498,8 @@
 
     @pl.when(has_prev)
     def _():
-        for piece in pieces[:3]:
+        for piece in pieces[:1]:
             piece.start()
-
-    store_grad = pltpu.make_async_copy(grad, grad_hbm, outs.at[0])
-    store_grad.start()
 
     def settle(ref, count, k):
         many = pltpu.make_async_remote_copy(
@@ -471,27 +507,38 @@
             dst_ref=ref.at[pl.ds(0, count)],
             send_sem=n_sem.at[k, 0],
             recv_sem=n_sem.at[k, 1],
-            device_id=group_peer(1),
+            device_id=z_peer(1),
             device_id_type=MESH,
         )
         return many
 
-    settle(n1, group - 1, 0).wait_recv()
-    n2[z] = jnp.sum(n1[...], axis=0)
-
-    def share2(d, carry):
-        share(n2, z, 1, z_peer(d)).start()
+    settle(n1, across - 1, 0).wait_recv()
+    n2[y] = jnp.sum(n1[...], axis=0)
+    for d in range(1, 4):
+        share(n2, y, 1, y_peer(d)).start()
+
+    @pl.when(has_prev)
+    def _():
+        for piece in pieces[1:3]:
+            piece.start()
+
+    z_wait(3)
+    settle(n2, 3, 1).wait_recv()
+    n3[z] = jnp.sum(n2[...], axis=0)
+
+    def share3(d, carry):
+        share(n3, z, 2, z_peer(d)).start()
         return carry
 
-    lax.fori_loop(1, depth, share2, 0)
+    lax.fori_loop(1, depth, share3, 0)
 
     @pl.when(has_prev)
     def _():
         for piece in pieces[3:]:
             piece.start()
 
-    settle(n2, depth - 1, 1).wait_recv()
-    sums = jnp.sum(n2[...], axis=0)
+    settle(n3, depth - 1, 2).wait_recv()
+    sums = jnp.sum(n3[...], axis=0)
     square_total = jnp.sum(jnp.where(lane < LANES // 2, sums, 0.0), axis=1, keepdims=True)
     cost_total = jnp.sum(jnp.where(lane < LANES // 2, 0.0, sums), axis=1, keepdims=True)
     cost_ref[...] = jnp.broadcast_to(0.5 * cost_total, (SUB, LANES))
@@ -522,8 +569,6 @@
 
         per_row(fn)
 
-    store_slid = pltpu.make_async_copy(slid, slid_hbm, outs.at[1])
-    store_slid.start()
     pl.when(has_north)(lambda: halo_up.wait_send())
     pl.when(has_south)(lambda: halo_down.wait_send())
     pl.when(has_north)(lambda: edge_up.wait_send())
@@ -531,8 +576,8 @@
 
     @pl.when(has_next)
     def _():
-        for c in range(3):
-            final[c].wait_send()
+        for piece in final:
+            piece.wait_send()
 
     @pl.when(has_prev)
     def _():
@@ -540,10 +585,21 @@
         for piece in pieces:
             piece.wait_send()
 
-    settle(n1, group - 1, 0).wait_send()
-    settle(n2, depth - 1, 1).wait_send()
-    store_grad.wait()
-    store_slid.wait()
+    settle(n1, across - 1, 0).wait_send()
+    settle(n2, 3, 1).wait_send()
+    settle(n3, depth - 1, 2).wait_send()
+
+
+def finish(slid, grad, cost, slid_hbm, grad_hbm, cost_ref, sem):
+    stores = [
+        pltpu.make_async_copy(slid, slid_hbm, sem.at[0]),
+        pltpu.make_async_copy(grad, grad_hbm, sem.at[1]),
+    ]
+    for store in stores:
+        store.start()
+    cost_ref[0, 0] = jnp.max(cost[...])
+    for store in stores:
+        store.wait()
 
 
 def to_tiles(x):
@@ -566,16 +622,15 @@
     high = rows + 2 * STEPS + 2
     vmem = lambda *shape: pltpu.VMEM(shape, jnp.float32)
     dma = pltpu.SemaphoreType.DMA
-    shape = jax.ShapeDtypeStruct((n, LANES), jnp.float32)
-    slid, grad, cost = pl.pallas_call(
+    held = pltpu.VMEM((n, LANES), jnp.float32)
+    stored = jax.ShapeDtypeStruct((n, LANES), jnp.float32)
+    whole = pl.BlockSpec(memory_space=pltpu.VMEM)
+    anywhere = pl.BlockSpec(memory_space=pl.ANY)
+    results = pl.pallas_call(
         functools.partial(kernel, windows, bands, rows, entries),
-        out_shape=(shape, shape, jax.ShapeDtypeStruct((SUB, LANES), jnp.float32)),
-        in_specs=[pl.BlockSpec(memory_space=pl.ANY)] * 4,
-        out_specs=(
-            pl.BlockSpec(memory_space=pl.ANY),
-            pl.BlockSpec(memory_space=pl.ANY),
-            pl.BlockSpec(memory_space=pltpu.VMEM),
-        ),
+        out_shape=(held, held, pltpu.VMEM((SUB, LANES), jnp.float32)),
+        in_specs=[anywhere] * 4,
+        out_specs=(whole, whole, whole),
         scratch_shapes=[
             vmem(n, LANES),
             vmem(n, LANES),
@@ -589,18 +644,18 @@
             vmem(3, rows, SUB, LANES),
             vmem(3, rows, SUB, LANES),
             vmem(2, 3, STEPS, SUB, LANES),
-            vmem(n, LANES),
-            vmem(n, LANES),
-            vmem(2 * bands, 1, LANES),
+            vmem(bands // 2, 1, LANES),
+            vmem(4, 1, LANES),
             vmem(windows // 2, 1, LANES),
             dma((4,)),
-            dma((2,)),
-            dma((8,)),
-            dma((8,)),
+            dma((5,)),
+            dma((5,)),
             dma((6,)),
             dma((6,)),
-            dma((2, 2)),
-            pltpu.SemaphoreType.REGULAR((3,)),
+            dma((6,)),
+            dma((6,)),
+            dma((3, 2)),
+            pltpu.SemaphoreType.REGULAR((4,)),
         ],
         compiler_params=pltpu.CompilerParams(collective_id=0, has_side_effects=True),
     )(
@@ -609,6 +664,13 @@
         to_tiles(observations[0]),
         to_tiles(obs_count[0]),
     )
+    slid, grad, cost = pl.pallas_call(
+        finish,
+        out_shape=(stored, stored, jax.ShapeDtypeStruct((1, 1), jnp.float32)),
+        in_specs=[whole] * 3,
+        out_specs=(anywhere, anywhere, pl.BlockSpec(memory_space=pltpu.SMEM)),
+        scratch_shapes=[dma((2,))],
+    )(*(pltpu.with_memory_space_constraint(r, pltpu.VMEM) for r in results))
     return (
         from_tiles(slid, rows, lon)[None],
         from_tiles(grad, rows, lon)[None],

time: 62.6 us -> 54.8 us (0.88)
  Pallas kernels: 58 us -> 54 us
  local copies, waits for them, and re-layouts: 3.75 us -> 0 us
    pallas_call x1, Pallas kernels: 58 us -> 52.6 us  [per_device(): pl.pallas_call(functools.partial(kernel, windows, bands, rows, entries),...]
    unnamed x4 -> x0, local copies, waits for them, and re-layouts: 2.57 us -> none
    pallas_call x0 -> x1, Pallas kernels: none -> 1.41 us  [per_device(): pl.pallas_call(finish, out_shape=(stored, stored, jax.ShapeDtypeStruct((1...]
    slice x1 -> x0, local copies, waits for them, and re-layouts: 1.18 us -> none  [per_device(): cost[0, 0]]
where the time goes in v2:
time: 54.8 us; the launch traced here: 54.7 us
  Pallas kernels  54 us (99%)
  between operations  0.64 us (1%)
    pallas_call x1, Pallas kernels, per_device(): pl.pallas_call(functools.partial(kernel, windows, bands, rows, entries),...  52.6 us
    pallas_call x1, Pallas kernels, per_device(): pl.pallas_call(finish, out_shape=(stored, stored, jax.ShapeDtypeStruct((1...  1.41 us

profile of v2, /device:TPU:1, one launch (start us, length us, event | category | flops | bytes accessed | tf_op | source)
XLA Modules:
  0.0 54.7 jit_solution(12828607098494520155)
XLA Ops:
  0.6 52.6 %shard_map.67 = (f32[768,128]{1,0:T(8,128)S(1)}, f32[768,128]{1,0:T(8,128)S(1)}, f32[8,128]{1,0:T(8,128)S(1)}) custom-call(f32[768,128]{1,0:T(8,128)} %bitcast.33, f32[768,128]{1,0:T(8,128)} %bitcast.34, f32[1024,128]{1,0:T(8,128)} %bitcast.31, s32[1024,128]{1,0:T(8,128)} %bitcast.32), custom_call_target="tpu_custom_call" | custom-call | tf_op jit(solution)/shard_map/pallas_call | solution.py:629
  53.3 1.4 %shard_map.68 = (f32[768,128]{1,0:T(8,128)}, f32[768,128]{1,0:T(8,128)}, f32[1,1]{1,0:T(1,128)}) custom-call(f32[768,128]{1,0:T(8,128)S(1)} %get-tuple-element.9.slid, f32[768,128]{1,0:T(8,128)S(1)} %get-tuple-element.10.grad, f32[8,128]{1,0:T(8,128)S(1)} %get-tuple-element.11.cost), custom_call_target="tpu_custom_call" | custom-call | tf_op jit(solution)/shard_map/pallas_call | solution.py:667

commit v3 on v2

--- a/solution.py
+++ b/solution.py
@@ -17,7 +17,8 @@
 STEPS = 4
 SUB, LANES = 8, 128
 BLOCK = 20
-EARLY, MIDDLE = 0, 3
+EARLY = 3
+PACE = 4
 MESH = pl.DeviceIdType.MESH
 
 
@@ -61,7 +62,6 @@
     edge,
     n1,
     n2,
-    n3,
     local,
     send,
     recv,
@@ -71,6 +71,7 @@
     a_recv,
     n_sem,
     z_sem,
+    x_sem,
 ):
     tm, lat = lax.axis_index("tm"), lax.axis_index("lat")
     z, y_hi = tm // 2, tm % 2
@@ -92,6 +93,14 @@
     def x_peer(d):
         i = lax.rem(slot + d, across)
         return at(tm, 4 * (i // 2) + 2 * y_lo + i % 2)
+
+    mine = y * across + slot
+    members = 4 * across
+
+    def plane_peer(d):
+        i = lax.rem(mine + d, members)
+        j, k = i // across, i % across
+        return at(2 * z + j // 2, 4 * (k // 2) + 2 * (j % 2) + k % 2)
 
     def y_peer(d):
         i = lax.rem(y + d, 4)
@@ -241,6 +250,8 @@
         pl.semaphore_wait(z_sem.at[k], (z + depth - d) // depth + (2 * depth - 1 - d - z) // depth)
 
     z_signal(0)
+    for d in range(1, across):
+        pl.semaphore_signal(x_sem, inc=1, device_id=x_peer(d), device_id_type=MESH)
     pl.when(has_south)(lambda: halo_up.wait_recv())
     pl.when(has_north)(lambda: halo_down.wait_recv())
 
@@ -281,11 +292,6 @@
     for j in range(STEPS):
         forward(j)
 
-    @pl.when(has_next)
-    def _():
-        for piece in final[:EARLY]:
-            piece.start()
-
     z_wait(0)
     z_signal(1)
 
@@ -306,10 +312,12 @@
     for j in range(STEPS):
         cost = per_row(observe(j), cost)
 
+    pl.when(has_prev)(lambda: control.wait_send())
+
     @pl.when(has_next)
     def _():
         control.wait_recv()
-        for piece in final[EARLY:MIDDLE]:
+        for piece in final[:EARLY]:
             piece.start()
 
         def start(t, r, carry):
@@ -411,7 +419,7 @@
 
     @pl.when(has_next)
     def _():
-        for piece in final[MIDDLE:]:
+        for piece in final[EARLY:]:
             piece.start()
 
     z_wait(1)
@@ -439,46 +447,6 @@
         edge_down.wait_recv()
         for c in range(3):
             L[p, c, top] = L[p, c, top] + edge[1, c]
-
-    @pl.when(has_prev)
-    def _():
-        for piece in final:
-            piece.wait_recv()
-
-    def gradient(t, r, carry):
-        squares, cost = carry
-        i = t * SUB + r
-        for c in range(3):
-            misfit = S[0, c, pad + i] - prev[c, i]
-            g = misfit + L[p, c, pad + i]
-            grad[tile_row(c, t, r), :] = g
-            squares = squares + g * g
-            cost = cost + misfit * misfit
-        return squares, cost
-
-    squares, cost = per_row(gradient, (zero, cost))
-
-    def fold(x):
-        x = jnp.sum(x, axis=0, keepdims=True)
-        return x + pltpu.roll(x, LANES // 2, 1)
-
-    lane = lax.broadcasted_iota(jnp.int32, (1, LANES), 1)
-    z_wait(2)
-    z_signal(3)
-    n1[slot] = jnp.where(lane < LANES // 2, fold(squares), fold(cost))
-
-    def share(ref, i, k, dev):
-        return pltpu.make_async_remote_copy(
-            src_ref=ref.at[i],
-            dst_ref=ref.at[i],
-            send_sem=n_sem.at[k, 0],
-            recv_sem=n_sem.at[k, 1],
-            device_id=dev,
-            device_id_type=MESH,
-        )
-
-    for d in range(1, across):
-        share(n1, slot, 0, x_peer(d)).start()
 
     pieces = []
     for q in range(2):
@@ -496,10 +464,63 @@
                 )
             )
 
+    def send_pieces(first, last):
+        @pl.when(has_prev)
+        def _():
+            for piece in pieces[first:last]:
+                piece.start()
+
+    z_wait(2)
+    z_signal(3)
+
     @pl.when(has_prev)
     def _():
-        for piece in pieces[:1]:
-            piece.start()
+        for piece in final:
+            piece.wait_recv()
+
+    def gradient(t, r, carry):
+        squares, cost = carry
+        i = t * SUB + r
+        for c in range(3):
+            misfit = S[0, c, pad + i] - prev[c, i]
+            g = misfit + L[p, c, pad + i]
+            grad[tile_row(c, t, r), :] = g
+            squares = squares + g * g
+            cost = cost + misfit * misfit
+        return squares, cost
+
+    squares, cost = per_row(gradient, (zero, cost))
+
+    def fold(x):
+        x = jnp.sum(x, axis=0, keepdims=True)
+        return x + pltpu.roll(x, LANES // 2, 1)
+
+    lane = lax.broadcasted_iota(jnp.int32, (1, LANES), 1)
+    pl.semaphore_wait(x_sem, across - 1)
+    n1[mine] = jnp.where(lane < LANES // 2, fold(squares), fold(cost))
+
+    def share(ref, i, k, dev):
+        return pltpu.make_async_remote_copy(
+            src_ref=ref.at[i],
+            dst_ref=ref.at[i],
+            send_sem=n_sem.at[k, 0],
+            recv_sem=n_sem.at[k, 1],
+            device_id=dev,
+            device_id_type=MESH,
+        )
+
+    def share1(d, carry):
+        share(n1, mine, 0, plane_peer(d)).start()
+        return carry
+
+    lax.fori_loop(1, members, share1, 0)
+
+    @pl.when(has_next)
+    def _():
+        for piece in final:
+            piece.wait_send()
+
+    send_pieces(0, PACE)
 
     def settle(ref, count, k):
         many = pltpu.make_async_remote_copy(
@@ -512,33 +533,18 @@
         )
         return many
 
-    settle(n1, across - 1, 0).wait_recv()
-    n2[y] = jnp.sum(n1[...], axis=0)
-    for d in range(1, 4):
-        share(n2, y, 1, y_peer(d)).start()
-
-    @pl.when(has_prev)
-    def _():
-        for piece in pieces[1:3]:
-            piece.start()
-
+    settle(n1, members - 1, 0).wait_recv()
+    n2[z] = jnp.sum(n1[...], axis=0)
     z_wait(3)
-    settle(n2, 3, 1).wait_recv()
-    n3[z] = jnp.sum(n2[...], axis=0)
-
-    def share3(d, carry):
-        share(n3, z, 2, z_peer(d)).start()
+
+    def share2(d, carry):
+        share(n2, z, 1, z_peer(d)).start()
         return carry
 
-    lax.fori_loop(1, depth, share3, 0)
-
-    @pl.when(has_prev)
-    def _():
-        for piece in pieces[3:]:
-            piece.start()
-
-    settle(n3, depth - 1, 2).wait_recv()
-    sums = jnp.sum(n3[...], axis=0)
+    lax.fori_loop(1, depth, share2, 0)
+    send_pieces(PACE, 6)
+    settle(n2, depth - 1, 1).wait_recv()
+    sums = jnp.sum(n2[...], axis=0)
     square_total = jnp.sum(jnp.where(lane < LANES // 2, sums, 0.0), axis=1, keepdims=True)
     cost_total = jnp.sum(jnp.where(lane < LANES // 2, 0.0, sums), axis=1, keepdims=True)
     cost_ref[...] = jnp.broadcast_to(0.5 * cost_total, (SUB, LANES))
@@ -574,20 +580,13 @@
     pl.when(has_north)(lambda: edge_up.wait_send())
     pl.when(has_south)(lambda: edge_down.wait_send())
 
-    @pl.when(has_next)
-    def _():
-        for piece in final:
-            piece.wait_send()
-
     @pl.when(has_prev)
     def _():
-        control.wait_send()
         for piece in pieces:
             piece.wait_send()
 
-    settle(n1, across - 1, 0).wait_send()
-    settle(n2, 3, 1).wait_send()
-    settle(n3, depth - 1, 2).wait_send()
+    settle(n1, members - 1, 0).wait_send()
+    settle(n2, depth - 1, 1).wait_send()
 
 
 def finish(slid, grad, cost, slid_hbm, grad_hbm, cost_ref, sem):
@@ -644,8 +643,7 @@
             vmem(3, rows, SUB, LANES),
             vmem(3, rows, SUB, LANES),
             vmem(2, 3, STEPS, SUB, LANES),
-            vmem(bands // 2, 1, LANES),
-            vmem(4, 1, LANES),
+            vmem(2 * bands, 1, LANES),
             vmem(windows // 2, 1, LANES),
             dma((4,)),
             dma((5,)),
@@ -654,8 +652,9 @@
             dma((6,)),
             dma((6,)),
             dma((6,)),
-            dma((3, 2)),
+            dma((2, 2)),
             pltpu.SemaphoreType.REGULAR((4,)),
+            pltpu.SemaphoreType.REGULAR,
         ],
         compiler_params=pltpu.CompilerParams(collective_id=0, has_side_effects=True),
     )(

time: 54.8 us -> 52.4 us (0.956)
  Pallas kernels: 54 us -> 51.6 us
    pallas_call x1, Pallas kernels: 52.6 us -> 50.2 us  [per_device(): pl.pallas_call(functools.partial(kernel, windows, bands, rows, entries),...]
where the time goes in v3:
time: 52.4 us; the launch traced here: 52.2 us
  Pallas kernels  51.6 us (98%)
  between operations  0.64 us (1%)
    pallas_call x1, Pallas kernels, per_device(): pl.pallas_call(functools.partial(kernel, windows, bands, rows, entries),...  50.2 us
    pallas_call x1, Pallas kernels, per_device(): pl.pallas_call(finish, out_shape=(stored, stored, jax.ShapeDtypeStruct((1...  1.41 us

profile of v3, /device:TPU:1, one launch (start us, length us, event | category | flops | bytes accessed | tf_op | source)
XLA Modules:
  0.0 52.2 jit_solution(14823284099808119902)
XLA Ops:
  0.6 50.2 %shard_map.67 = (f32[768,128]{1,0:T(8,128)S(1)}, f32[768,128]{1,0:T(8,128)S(1)}, f32[8,128]{1,0:T(8,128)S(1)}) custom-call(f32[768,128]{1,0:T(8,128)} %bitcast.33, f32[768,128]{1,0:T(8,128)} %bitcast.34, f32[1024,128]{1,0:T(8,128)} %bitcast.31, s32[1024,128]{1,0:T(8,128)} %bitcast.32), custom_call_target="tpu_custom_call" | custom-call | tf_op jit(solution)/shard_map/pallas_call | solution.py:628
  50.8 1.4 %shard_map.68 = (f32[768,128]{1,0:T(8,128)}, f32[768,128]{1,0:T(8,128)}, f32[1,1]{1,0:T(1,128)}) custom-call(f32[768,128]{1,0:T(8,128)S(1)} %get-tuple-element.9.slid, f32[768,128]{1,0:T(8,128)S(1)} %get-tuple-element.10.grad, f32[8,128]{1,0:T(8,128)S(1)} %get-tuple-element.11.cost), custom_call_target="tpu_custom_call" | custom-call | tf_op jit(solution)/shard_map/pallas_call | solution.py:666

commit v4 on v3

--- a/solution.py
+++ b/solution.py
@@ -17,6 +17,7 @@
 STEPS = 4
 SUB, LANES = 8, 128
 BLOCK = 20
+CHUNKS = 3
 EARLY = 3
 PACE = 4
 MESH = pl.DeviceIdType.MESH
@@ -45,8 +46,10 @@
     bg_hbm,
     obs_hbm,
     cnt_hbm,
-    slid,
+    start_ref,
+    slope,
     grad,
+    scale_ref,
     cost_ref,
     xin,
     bg,
@@ -314,11 +317,14 @@
 
     pl.when(has_prev)(lambda: control.wait_send())
 
-    @pl.when(has_next)
-    def _():
-        control.wait_recv()
+    @pl.when(has_next & (y_hi == 0))
+    def _():
         for piece in final[:EARLY]:
             piece.start()
+
+    @pl.when(has_next)
+    def _():
+        control.wait_recv()
 
         def start(t, r, carry):
             i = t * SUB + r
@@ -330,6 +336,11 @@
             return carry
 
         per_row(start)
+
+    @pl.when(has_next & (y_hi == 1))
+    def _():
+        for piece in final[:EARLY]:
+            piece.start()
 
     @pl.when(jnp.logical_not(has_next))
     def _():
@@ -543,38 +554,39 @@
 
     lax.fori_loop(1, depth, share2, 0)
     send_pieces(PACE, 6)
+
+    @pl.when(has_next)
+    def _():
+        for piece in pieces:
+            piece.wait_recv()
+
+        def fn(t, r, carry):
+            i = t * SUB + r
+            for c in range(3):
+                control = fol[tile_row(c, t, r), :]
+                start_ref[tile_row(c, t, r), :] = control
+                slope[tile_row(c, t, r), :] = (control - S[STEPS, c, pad + i]) + adjn[c, i]
+            return carry
+
+        per_row(fn)
+
+    @pl.when(jnp.logical_not(has_next))
+    def _():
+        def fn(t, r, carry):
+            for c in range(3):
+                start_ref[tile_row(c, t, r), :] = S[STEPS, c, pad + t * SUB + r]
+                slope[tile_row(c, t, r), :] = row_tile
+            return carry
+
+        per_row(fn)
+
     settle(n2, depth - 1, 1).wait_recv()
     sums = jnp.sum(n2[...], axis=0)
     square_total = jnp.sum(jnp.where(lane < LANES // 2, sums, 0.0), axis=1, keepdims=True)
     cost_total = jnp.sum(jnp.where(lane < LANES // 2, 0.0, sums), axis=1, keepdims=True)
     cost_ref[...] = jnp.broadcast_to(0.5 * cost_total, (SUB, LANES))
     scale = step_scale / jnp.sqrt(square_total / entries + epsilon)
-    scale = jnp.broadcast_to(scale, (SUB, LANES))
-
-    @pl.when(has_next)
-    def _():
-        for piece in pieces:
-            piece.wait_recv()
-
-        def fn(t, r, carry):
-            i = t * SUB + r
-            for c in range(3):
-                control = fol[tile_row(c, t, r), :]
-                g = (control - S[STEPS, c, pad + i]) + adjn[c, i]
-                slid[tile_row(c, t, r), :] = control - scale * g
-            return carry
-
-        per_row(fn)
-
-    @pl.when(jnp.logical_not(has_next))
-    def _():
-        def fn(t, r, carry):
-            for c in range(3):
-                slid[tile_row(c, t, r), :] = S[STEPS, c, pad + t * SUB + r]
-            return carry
-
-        per_row(fn)
-
+    scale_ref[...] = jnp.broadcast_to(scale, (SUB, LANES))
     pl.when(has_north)(lambda: halo_up.wait_send())
     pl.when(has_south)(lambda: halo_down.wait_send())
     pl.when(has_north)(lambda: edge_up.wait_send())
@@ -589,16 +601,21 @@
     settle(n2, depth - 1, 1).wait_send()
 
 
-def finish(slid, grad, cost, slid_hbm, grad_hbm, cost_ref, sem):
-    stores = [
-        pltpu.make_async_copy(slid, slid_hbm, sem.at[0]),
-        pltpu.make_async_copy(grad, grad_hbm, sem.at[1]),
-    ]
-    for store in stores:
-        store.start()
+def finish(start, slope, grad, scale, cost, slid_hbm, grad_hbm, cost_ref, slid, sem):
+    store_grad = pltpu.make_async_copy(grad, grad_hbm, sem.at[CHUNKS])
+    store_grad.start()
+    rows = slid.shape[0] // CHUNKS
+    s = jnp.broadcast_to(scale[0:1], (rows, LANES))
+    stores = []
+    for q in range(CHUNKS):
+        part = pl.ds(q * rows, rows)
+        slid[part] = start[part] - s * slope[part]
+        stores.append(pltpu.make_async_copy(slid.at[part], slid_hbm.at[part], sem.at[q]))
+        stores[-1].start()
     cost_ref[0, 0] = jnp.max(cost[...])
     for store in stores:
         store.wait()
+    store_grad.wait()
 
 
 def to_tiles(x):
@@ -622,14 +639,15 @@
     vmem = lambda *shape: pltpu.VMEM(shape, jnp.float32)
     dma = pltpu.SemaphoreType.DMA
     held = pltpu.VMEM((n, LANES), jnp.float32)
+    tile = pltpu.VMEM((SUB, LANES), jnp.float32)
     stored = jax.ShapeDtypeStruct((n, LANES), jnp.float32)
     whole = pl.BlockSpec(memory_space=pltpu.VMEM)
     anywhere = pl.BlockSpec(memory_space=pl.ANY)
     results = pl.pallas_call(
         functools.partial(kernel, windows, bands, rows, entries),
-        out_shape=(held, held, pltpu.VMEM((SUB, LANES), jnp.float32)),
+        out_shape=(held, held, held, tile, tile),
         in_specs=[anywhere] * 4,
-        out_specs=(whole, whole, whole),
+        out_specs=(whole,) * 5,
         scratch_shapes=[
             vmem(n, LANES),
             vmem(n, LANES),
@@ -666,9 +684,9 @@
     slid, grad, cost = pl.pallas_call(
         finish,
         out_shape=(stored, stored, jax.ShapeDtypeStruct((1, 1), jnp.float32)),
-        in_specs=[whole] * 3,
+        in_specs=[whole] * 5,
         out_specs=(anywhere, anywhere, pl.BlockSpec(memory_space=pltpu.SMEM)),
-        scratch_shapes=[dma((2,))],
+        scratch_shapes=[vmem(n, LANES), dma((CHUNKS + 1,))],
     )(*(pltpu.with_memory_space_constraint(r, pltpu.VMEM) for r in results))
     return (
         from_tiles(slid, rows, lon)[None],

time: 52.4 us -> 51.9 us (level)
  no operation moved by 1% of the time
where the time goes in v4:
time: 51.9 us; the launch traced here: 51.8 us
  Pallas kernels  51.1 us (98%)
  between operations  0.64 us (1%)
    pallas_call x1, Pallas kernels, per_device(): pl.pallas_call(functools.partial(kernel, windows, bands, rows, entries),...  49.7 us
    pallas_call x1, Pallas kernels, per_device(): pl.pallas_call(finish, out_shape=(stored, stored, jax.ShapeDtypeStruct((1...  1.43 us

profile of v4, /device:TPU:1, one launch (start us, length us, event | category | flops | bytes accessed | tf_op | source)
XLA Modules:
  0.0 51.8 jit_solution(9296466227996686771)
XLA Ops:
  0.6 49.7 %shard_map.67 = (f32[768,128]{1,0:T(8,128)S(1)}, f32[768,128]{1,0:T(8,128)S(1)}, f32[768,128]{1,0:T(8,128)S(1)}, f32[8,128]{1,0:T(8,128)S(1)}, f32[8,128]{1,0:T(8,128)S(1)}) custom-call(f32[768,128]{1,0:T(8,128)} %bitcast.33, f32[768,128]{1,0:T(8,128)} %bitcast.34, f32[1024,128]{1,0:T(8,128)} %bitcast.31, s32[1024,128]{1,0:T(8,128)} %bitcast.32), custom_call_target="tpu_custom_call" | custom-call | tf_op jit(solution)/shard_map/pallas_call | solution.py:646
  50.3 1.4 %shard_map.68 = (f32[768,128]{1,0:T(8,128)}, f32[768,128]{1,0:T(8,128)}, f32[1,1]{1,0:T(1,128)}) custom-call(f32[768,128]{1,0:T(8,128)S(1)} %get-tuple-element.11.start, f32[768,128]{1,0:T(8,128)S(1)} %get-tuple-element.12.slope, f32[768,128]{1,0:T(8,128)S(1)} %get-tuple-element.13.grad, f32[8,128]{1,0:T(8,128)S(1)} %get-tuple-element.14.scale, ...), custom_call_target="tpu_custom_call" | custom-call | tf_op jit(solution)/shard_map/pallas_call | solution.py:684

commit v5 on v4

--- a/solution.py
+++ b/solution.py
@@ -102,8 +102,9 @@
 
     def plane_peer(d):
         i = lax.rem(mine + d, members)
-        j, k = i // across, i % across
-        return at(2 * z + j // 2, 4 * (k // 2) + 2 * (j % 2) + k % 2)
+        j, k = lax.div(i, across), lax.rem(i, across)
+        x_core = lax.rem(k, 2) + 4 * lax.div(k, 2)
+        return at(2 * z + lax.div(j, 2), x_core + 2 * lax.rem(j, 2))
 
     def y_peer(d):
         i = lax.rem(y + d, 4)
@@ -319,7 +320,7 @@
 
     @pl.when(has_next & (y_hi == 0))
     def _():
-        for piece in final[:EARLY]:
+        for piece in final:
             piece.start()
 
     @pl.when(has_next)
@@ -428,7 +429,7 @@
     pl.when(has_north)(lambda: edge_up.start())
     pl.when(has_south)(lambda: edge_down.start())
 
-    @pl.when(has_next)
+    @pl.when(has_next & (y_hi == 1))
     def _():
         for piece in final[EARLY:]:
             piece.start()

time: 51.9 us -> 51.3 us (0.988)
    pallas_call x1, Pallas kernels: 49.7 us -> 49.1 us  [per_device(): pl.pallas_call(functools.partial(kernel, windows, bands, rows, entries),...]
where the time goes in v5:
time: 51.3 us; the launch traced here: 51.2 us
  Pallas kernels  50.6 us (99%)
  between operations  0.64 us (1%)
    pallas_call x1, Pallas kernels, per_device(): pl.pallas_call(functools.partial(kernel, windows, bands, rows, entries),...  49.1 us
    pallas_call x1, Pallas kernels, per_device(): pl.pallas_call(finish, out_shape=(stored, stored, jax.ShapeDtypeStruct((1...  1.43 us

profile of v5, /device:TPU:1, one launch (start us, length us, event | category | flops | bytes accessed | tf_op | source)
XLA Modules:
  0.0 51.2 jit_solution(3798616009759513232)
XLA Ops:
  0.6 49.1 %shard_map.67 = (f32[768,128]{1,0:T(8,128)S(1)}, f32[768,128]{1,0:T(8,128)S(1)}, f32[768,128]{1,0:T(8,128)S(1)}, f32[8,128]{1,0:T(8,128)S(1)}, f32[8,128]{1,0:T(8,128)S(1)}) custom-call(f32[768,128]{1,0:T(8,128)} %bitcast.33, f32[768,128]{1,0:T(8,128)} %bitcast.34, f32[1024,128]{1,0:T(8,128)} %bitcast.31, s32[1024,128]{1,0:T(8,128)} %bitcast.32), custom_call_target="tpu_custom_call" | custom-call | tf_op jit(solution)/shard_map/pallas_call | solution.py:647
  49.8 1.4 %shard_map.68 = (f32[768,128]{1,0:T(8,128)}, f32[768,128]{1,0:T(8,128)}, f32[1,1]{1,0:T(1,128)}) custom-call(f32[768,128]{1,0:T(8,128)S(1)} %get-tuple-element.11.start, f32[768,128]{1,0:T(8,128)S(1)} %get-tuple-element.12.slope, f32[768,128]{1,0:T(8,128)S(1)} %get-tuple-element.13.grad, f32[8,128]{1,0:T(8,128)S(1)} %get-tuple-element.14.scale, ...), custom_call_target="tpu_custom_call" | custom-call | tf_op jit(solution)/shard_map/pallas_call | solution.py:685
